TPU v7x, 32 devices: a whole 2x2x4 slice. The times are simulated.
32 devices in a mesh: leaf: 4 (over x, core), ctx: 8 (over z, y).
Axes of the slice: x: 2, y: 2, z: 4, core: 2. Of those that a mesh axis runs over, the one named last changes fastest.
Arguments:
- queries: bfloat16 [4096, 4096], P(('leaf', 'ctx')), parts along dimension 0, may hold values from -6 to 6
- keys: bfloat16 [4096, 512], P(('leaf', 'ctx')), parts along dimension 0, may hold values from -6 to 6
- values: bfloat16 [4096, 512], P(('leaf', 'ctx')), parts along dimension 0, may hold values from -6 to 6
- grad_out: bfloat16 [4096, 4096], P(('leaf', 'ctx')), parts along dimension 0, may hold values from -6 to 6
- block_path: int32 [32, 4], P('leaf'), parts along dimension 0, may hold values from -1 to 7, as said below
- assistant: int32 [4096], P(('leaf', 'ctx')), parts along dimension 0, may hold values from 0 to 1, as said below
Outputs:
- attention: bfloat16 [4096, 4096], P(('leaf', 'ctx')), parts along dimension 0
- grad_queries: bfloat16 [4096, 4096], P(('leaf', 'ctx')), parts along dimension 0
- grad_keys: bfloat16 [4096, 512], P(('leaf', 'ctx')), parts along dimension 0
- grad_values: bfloat16 [4096, 512], P(('leaf', 'ctx')), parts along dimension 0
There are 4 independent parts, one for each index of `leaf`. A program takes and returns all parts, laid end to end along the dimension named above; each array names one. Nothing has to cross between parts.
Inputs may be any that keep to these rules, and one draw needn't show every extreme that they name: `block_path`: blocks lie in depth-first order of the tree; every node spans one block; block 0 is the root at depth 0. Row b holds at depth e <= depth(b) the block of b's ancestor node at that depth (b itself at e = depth(b)) and -1 below. `assistant`: each block of 128 tokens holds one run of ones.
All inputs are finite; a program needn't handle non-finite values.
Results may differ from a plain program's by a relative error of at most 0.0091.
Values may be sent and summed in bfloat16 or wider, within the bound.
No kernel may reach another device: no remote copies, remote signals or barrier semaphores. Data moves between devices by JAX's collectives and lax.ppermute only.
A program may use at most 128 MiB of HBM per device.

v0:
```python
import math
import jax
import jax.numpy as jnp
from jax import lax
from jax.sharding import PartitionSpec as P

KEY_HEADS = 4
HEAD_WIDTH = 128
HEADS_PER_KEY = 8


def prefix(x, axis, combine, identity):
    size, here = (lax.axis_size(axis), lax.axis_index(axis))
    everything = jax.tree.map(lambda part: lax.all_gather(part, axis), x)
    start = jax.tree.map(
        lambda part, zero: jnp.broadcast_to(jnp.asarray(zero, part.dtype), part.shape), x, identity
    )

    def hop(k, before):
        at = size - 1 - k
        reached = at > here
        new = combine(before, jax.tree.map(lambda part: part[at], everything))
        return jax.tree.map(lambda a, b: jnp.where(reached, a, b), new, before)

    return lax.fori_loop(0, size, hop, start)


def dot_rows(left, right):
    return lax.dot_general(
        left, right, (((1,), (1,)), ((), ())), preferred_element_type=jnp.float32
    )


def dot_cols(left, right):
    return lax.dot_general(
        left, right, (((0,), (0,)), ((), ())), preferred_element_type=jnp.float32
    )


def attend_block(queries, grad_rows, slot_keys, slot_values, allowed):
    block_rows = queries.shape[0]
    head_cols = HEADS_PER_KEY * HEAD_WIDTH
    scaling = 1.0 / math.sqrt(HEAD_WIDTH)
    wide_mask = jnp.repeat(allowed, HEADS_PER_KEY, axis=0)
    attended_parts, query_parts, key_parts, value_parts = ([], [], [], [])
    for key_value_head in range(KEY_HEADS):
        query_matrix = queries[
            :, key_value_head * head_cols : (key_value_head + 1) * head_cols
        ].reshape(block_rows * HEADS_PER_KEY, HEAD_WIDTH)
        grad_head = grad_rows[
            :, key_value_head * head_cols : (key_value_head + 1) * head_cols
        ].reshape(block_rows * HEADS_PER_KEY, HEAD_WIDTH)
        key_cols = slot_keys[:, key_value_head * HEAD_WIDTH : (key_value_head + 1) * HEAD_WIDTH]
        value_cols = slot_values[:, key_value_head * HEAD_WIDTH : (key_value_head + 1) * HEAD_WIDTH]
        scores = jnp.where(wide_mask, dot_rows(query_matrix, key_cols) * scaling, -jnp.inf)
        row_max = jnp.max(scores, axis=1, keepdims=True)
        row_sum = jnp.sum(jnp.exp(scores - row_max), axis=1, keepdims=True)
        log_total = row_max + jnp.log(row_sum)
        rounded = jnp.exp(scores - log_total).astype(jnp.bfloat16)
        attended = jnp.dot(rounded, value_cols, preferred_element_type=jnp.float32).astype(
            jnp.bfloat16
        )
        attended = lax.optimization_barrier(attended)
        row_delta = jnp.sum(
            grad_head.astype(jnp.float32) * attended.astype(jnp.float32), axis=1, keepdims=True
        )
        grad_prob = dot_rows(grad_head, value_cols)
        grad_score = (jnp.exp(scores - log_total) * (grad_prob - row_delta)).astype(jnp.bfloat16)
        grad_query = (
            jnp.dot(grad_score, key_cols, preferred_element_type=jnp.float32) * scaling
        ).astype(jnp.bfloat16)
        grad_key = dot_cols(grad_score, query_matrix) * scaling
        grad_value = dot_cols(rounded, grad_head)
        attended_parts.append(attended.reshape(block_rows, head_cols))
        query_parts.append(grad_query.reshape(block_rows, head_cols))
        key_parts.append(grad_key)
        value_parts.append(grad_value)
    return (
        jnp.concatenate(attended_parts, 1),
        jnp.concatenate(query_parts, 1),
        jnp.concatenate(key_parts, 1),
        jnp.concatenate(value_parts, 1),
    )


def on_device(queries, keys, values, grad_out, block_path, assistant):
    block_rows = queries.shape[0]
    kv_width = keys.shape[1]
    position = lax.axis_index("ctx")
    depths = jnp.sum((block_path >= 0).astype(jnp.int32), axis=1) - 1
    own_path = lax.dynamic_index_in_dim(block_path, position, 0, keepdims=False)
    own_depth = lax.dynamic_index_in_dim(depths, position, 0, keepdims=False)
    seen_slots = jnp.stack([own_depth > 0, own_depth > 1, own_depth > 2])
    wanted_blocks = jnp.stack([own_path[0], own_path[1], own_path[2]])
    row_ids = jnp.arange(block_rows, dtype=jnp.int32)
    empty = jnp.zeros((3, block_rows, kv_width), jnp.bfloat16)
    picked = (empty, empty)
    key_piece = lax.all_gather(keys, "ctx", axis=0, tiled=True)
    value_piece = lax.all_gather(values, "ctx", axis=0, tiled=True)
    piece_rows = key_piece.shape[0]
    for slot_number in range(3):
        wanted = wanted_blocks[slot_number]
        begin = wanted * block_rows
        touches = (wanted >= 0) & (begin < piece_rows) & (begin + block_rows > 0)

        def fill(current, slot_number=slot_number, begin=begin):
            local_rows = begin + row_ids
            inside = (local_rows >= 0) & (local_rows < piece_rows)
            clipped = jnp.clip(local_rows, 0, piece_rows - 1)
            new_keys = jnp.where(inside[:, None], key_piece[clipped], current[0][slot_number])
            new_values = jnp.where(inside[:, None], value_piece[clipped], current[1][slot_number])
            return (
                current[0].at[slot_number].set(new_keys),
                current[1].at[slot_number].set(new_values),
            )

        def unchanged(current):
            return current

        picked = lax.cond(touches, fill, unchanged, picked)
    far_keys, far_values = picked
    slot_keys = jnp.concatenate([far_keys.reshape(3 * block_rows, kv_width), keys], 0)
    slot_values = jnp.concatenate([far_values.reshape(3 * block_rows, kv_width), values], 0)
    full_slots = jnp.repeat(seen_slots, block_rows)
    causal = jnp.arange(block_rows)[:, None] >= jnp.arange(block_rows)[None, :]
    allowed = jnp.concatenate(
        [jnp.broadcast_to(full_slots[None, :], (block_rows, 3 * block_rows)), causal], 1
    )
    grad_rows = grad_out * assistant[:, None].astype(jnp.bfloat16)
    attention, grad_queries, grad_key_all, grad_value_all = attend_block(
        queries, grad_rows, slot_keys, slot_values, allowed
    )
    slot_grads = jnp.stack(
        [
            grad_key_all.reshape(4, block_rows, kv_width),
            grad_value_all.reshape(4, block_rows, kv_width),
        ],
        1,
    )
    grad_total = slot_grads[3]
    tree_depths = [0, 1, 2]
    resets = jnp.stack([own_depth <= tree_level for tree_level in tree_depths]).astype(jnp.float32)
    carried = jnp.stack([slot_grads[tree_level] for tree_level in tree_depths])

    def accumulate(earlier, latter):
        marker = jnp.maximum(earlier[0], latter[0])
        summed = jnp.where(latter[0][:, None, None, None] > 0.5, latter[1], earlier[1] + latter[1])
        return (marker, summed)

    identity = (jnp.zeros_like(resets), jnp.zeros_like(carried))
    _, received = prefix((resets, carried), "ctx", accumulate, identity)
    for slot_index, tree_level in enumerate(tree_depths):
        grad_total = grad_total + jnp.where(own_depth == tree_level, received[slot_index], 0.0)
    return (
        attention,
        grad_queries,
        grad_total[0].astype(jnp.bfloat16),
        grad_total[1].astype(jnp.bfloat16),
    )


def solution(mesh):
    in_specs = (
        P(("leaf", "ctx"), None),
        P(("leaf", "ctx"), None),
        P(("leaf", "ctx"), None),
        P(("leaf", "ctx"), None),
        P("leaf", None),
        P(("leaf", "ctx")),
    )
    out_specs = (
        P(("leaf", "ctx"), None),
        P(("leaf", "ctx"), None),
        P(("leaf", "ctx"), None),
        P(("leaf", "ctx"), None),
    )
    return jax.shard_map(
        on_device, mesh=mesh, in_specs=in_specs, out_specs=out_specs, check_vma=False
    )
```

profile of v0, /device:TPU:0, one launch (start us, length us, event | category | flops | bytes accessed | tf_op | source)
XLA Modules:
  0.0 329.6 jit_solution(16792930033362038903)
XLA Ops:
  19.0 1.1 reshape.481
  23.4 29.8 %all-gather.6.cloned.1.call-done = bf16[1024,512]{1,0:T(8,128)(2,1)} async-done(((bf16[128,512]{1,0:T(8,128)(2,1)}), bf16[1024,512]{1,0:T(8,128)(2,1)}) %all-gather.6.cloned.1.call-update) | async-done | bytes 1048592 | tf_op jit(solution)/shard_map/all_gather | solution.py:98
  53.2 41.1 %all-gather.8.cloned.1.call-done = bf16[1024,512]{1,0:T(8,128)(2,1)} async-done(((bf16[128,512]{1,0:T(8,128)(2,1)}), bf16[1024,512]{1,0:T(8,128)(2,1)}) %all-gather.8.cloned.1.call-update) | async-done | bytes 1048592 | tf_op jit(solution)/shard_map/all_gather | solution.py:99
  94.3 4.7 %conditional.3 = (bf16[3,128,512]{2,1,0:T(8,128)(2,1)S(1)}, bf16[3,128,512]{2,1,0:T(8,128)(2,1)S(1)}) conditional(s32[]{:T(128)} %convert_element_type.109, () %tuple.88, (s32[]{:T(128)}, s32[128]{0:T(128)S(1)}, bf16[1024,512]{1,0:T(8,128)(2,1)}, bf16[1024,512]{1,0:T(8,128)(2,1)}) %tuple.89), branch_computations={%region_1.2_spmd, %region_2.3_spmd} | conditional | flops 133248 | bytes 2104604 | solution.py:120
  94.3 2.2 gather_fusion.1
  96.6 2.2 gather_fusion
  109.2 1.5 multiply_convert_fusion.2
  111.4 1.5 multiply_convert_fusion.3
  113.0 1.1 pad_maximum_fusion.4
  114.0 1.6 copy.47
  116.2 1.7 convolution_multiply_fusion.5
  119.3 1.3 pad_maximum_fusion
  122.8 24.4 %all-gather.1 = f32[8,1,3]{2,1,0:T(1,128)S(1)} all-gather(f32[1,1,3]{2,1,0:T(1,128)S(1)} %fusion.44), channel_id=1, replica_groups=mesh['leaf'=4,'ctx'=8] {'ctx'}, dimensions={0}, use_global_device_ids=true | all-gather | bytes 108 | tf_op jit(solution)/shard_map/all_gather | solution.py:14
  150.0 1.8 reshape.480
  151.8 1.8 reshape.478
  153.5 1.8 reshape.476
  155.3 1.7 fusion.12
  157.8 1.7 fusion.11
  160.4 1.7 fusion.10
  162.9 1.7 fusion.9
  165.5 2.3 pad_maximum_fusion.1
  168.9 135.4 %all-gather.10.cloned.1.call-done = f32[24,2,128,512]{3,2,1,0:T(8,128)} async-done(((f32[3,2,128,512]{3,2,1,0:T(8,128)}), f32[24,2,128,512]{3,2,1,0:T(8,128)}) %all-gather.10.cloned.1.call-update) | async-done | bytes 12582928 | tf_op jit(solution)/shard_map/all_gather | solution.py:14
  304.3 16.8 %while.22 = (s32[]{:T(128)}, f32[3,2,128,512]{3,2,1,0:T(8,128)S(1)}, s32[]{:T(128)}, f32[8,3]{1,0:T(8,128)S(1)}, f32[8,3,2,128,512]{4,3,2,1,0:T(8,128)}, /*index=5*/s32[]{:T(128)}, s32[]{:T(128)}, s32[]{:T(128)}, s32[]{:T(128)}) while((s32[]{:T(128)}, f32[3,2,128,512]{3,2,1,0:T(8,128)S(1)}, s32[]{:T(128)}, ...), condition=%wide.region_20.21_spmd.clone, body=%wide.region_19.20_spmd.clone.sunk | while | flops 1572875 | bytes 4718785 | solution.py:25
  304.3 2.0 fusion.77
  306.4 2.1 fusion.77
  308.5 2.1 fusion.77
  310.6 2.1 fusion.77
  312.8 2.1 fusion.77
  314.9 2.1 fusion.77
  317.0 2.1 fusion.77
  319.1 2.1 fusion.77
  321.1 1.2 fusion.15
  (147 shorter events, 28.0 us)
Async XLA Ops:
  7.2 11.1 %copy-start.20 = (bf16[128,4096]{1,0:T(8,128)(2,1)S(1)}, bf16[128,4096]{1,0:T(8,128)(2,1)}, u32[]{:S(2)}) copy-start(bf16[128,4096]{1,0:T(8,128)(2,1)} %param.26) | copy-start | bytes 3145732
  7.2 46.0 %all-gather.6.cloned.1.call-start = ((), (), s32[]{:S(2)}) async-start(), calls=%async_computation | async-start | bytes 1179648 | tf_op jit(solution)/shard_map/all_gather | solution.py:98
  7.9 86.4 %all-gather.8.cloned.1.call-start = ((), (), s32[]{:S(2)}) async-start(), calls=%async_computation.1 | async-start | bytes 1179648 | tf_op jit(solution)/shard_map/all_gather | solution.py:99
  8.7 295.7 %all-gather.10.cloned.1.call-start = ((), (), s32[]{:S(2)}) async-start(), calls=%async_computation.2 | async-start | bytes 14155776 | tf_op jit(solution)/shard_map/all_gather | solution.py:14
  18.2 4.4 %copy-start.27 = (s32[128]{0:T(128)S(1)}, s32[128]{0:T(128)}, u32[]{:S(2)}) copy-start(s32[128]{0:T(128)} %param.31) | copy-start | bytes 1540
  18.2 4.4 %copy-start.19 = (bf16[128,4096]{1,0:T(8,128)(2,1)S(1)}, bf16[128,4096]{1,0:T(8,128)(2,1)}, u32[]{:S(2)}) copy-start(bf16[128,4096]{1,0:T(8,128)(2,1)} %param.29) | copy-start | bytes 3145732
  20.1 79.8 %copy-start.12 = (bf16[1024,128]{1,0:T(8,128)(2,1)}, bf16[1024,128]{1,0:T(8,128)(2,1)S(1)}, u32[]{:S(2)}) copy-start(bf16[1024,128]{1,0:T(8,128)(2,1)S(1)} %reshape.481) | copy-start | bytes 786436
  99.0 0.9 copy-start.25
  100.0 4.5 %copy-start.5 = (bf16[512,512]{1,0:T(8,128)(2,1)}, bf16[512,512]{1,0:T(8,128)(2,1)S(1)}, u32[]{:S(2)}) copy-start(bf16[512,512]{1,0:T(8,128)(2,1)S(1)} %constant_dynamic-update-slice_fusion) | copy-start | bytes 1572868
  100.0 1.0 copy-start.26
  100.5 1.1 copy-start.14
  101.6 4.9 %copy-start.7 = (bf16[1024,128]{1,0:T(8,128)(2,1)}, bf16[1024,128]{1,0:T(8,128)(2,1)S(1)}, u32[]{:S(2)}) copy-start(bf16[1024,128]{1,0:T(8,128)(2,1)S(1)} %convolution_convert_fusion) | copy-start | bytes 786436
  102.1 1.0 copy-start.15
  103.1 4.7 %copy-start.9 = (bf16[1024,128]{1,0:T(8,128)(2,1)}, bf16[1024,128]{1,0:T(8,128)(2,1)S(1)}, u32[]{:S(2)}) copy-start(bf16[1024,128]{1,0:T(8,128)(2,1)S(1)} %convolution_convert_fusion.1) | copy-start | bytes 786436
  103.6 1.0 copy-start.17
  104.5 4.5 %copy-start.10 = (bf16[1024,128]{1,0:T(8,128)(2,1)}, bf16[1024,128]{1,0:T(8,128)(2,1)S(1)}, u32[]{:S(2)}) copy-start(bf16[1024,128]{1,0:T(8,128)(2,1)S(1)} %convolution_convert_fusion.2) | copy-start | bytes 786436
  105.9 5.3 %copy-start.11 = (bf16[1024,128]{1,0:T(8,128)(2,1)}, bf16[1024,128]{1,0:T(8,128)(2,1)S(1)}, u32[]{:S(2)}) copy-start(bf16[1024,128]{1,0:T(8,128)(2,1)S(1)} %convolution_convert_fusion.3) | copy-start | bytes 786436
  107.2 8.4 %copy-start.1 = (bf16[1024,512]{0,1:T(8,128)(2,1)}, bf16[1024,512]{0,1:T(8,128)(2,1)S(1)}, u32[]{:S(2)}) copy-start(bf16[1024,512]{0,1:T(8,128)(2,1)S(1)} %multiply_convert_fusion) | copy-start | bytes 3145732
  108.5 7.7 %copy-start.2 = (bf16[1024,512]{0,1:T(8,128)(2,1)}, bf16[1024,512]{0,1:T(8,128)(2,1)S(1)}, u32[]{:S(2)}) copy-start(bf16[1024,512]{0,1:T(8,128)(2,1)S(1)} %multiply_convert_fusion.1) | copy-start | bytes 3145732
  113.0 2.6 copy-start.13
  115.6 2.2 copy-start.3
  115.6 2.2 copy-start.16
  115.6 2.7 copy-start.4
  115.6 2.7 copy-start.18
  119.3 1.5 copy-start
  119.3 29.8 %copy-start.8 = (bf16[1024,128]{1,0:T(8,128)(2,1)S(1)}, bf16[1024,128]{1,0:T(8,128)(2,1)}, u32[]{:S(2)}) copy-start(bf16[1024,128]{1,0:T(8,128)(2,1)} %copy-done.7) | copy-start | bytes 786436
  120.6 34.7 %copy-start.6 = (bf16[512,512]{1,0:T(8,128)(2,1)S(1)}, bf16[512,512]{1,0:T(8,128)(2,1)}, u32[]{:S(2)}) copy-start(bf16[512,512]{1,0:T(8,128)(2,1)} %copy-done.5) | copy-start | bytes 1572868
  164.6 3.2 copy-start.21
  164.7 3.2 copy-start.22
  165.5 2.3 copy-start.23
  165.5 2.3 copy-start.24
Sparse Core Ops, SparseCore 0:
  10.1 43.0 all-gather.5
  55.3 38.9 all-gather.7
  120.7 183.5 all-gather.9
where the time goes:
time: 331 us; the launch traced here: 330 us
  waiting for transfers between devices  208 us (63%)
  other arithmetic  26.8 us (8%)
  local copies, waits for them, and re-layouts  25.5 us (8%)
  blocking collectives  24.4 us (7%)
  between operations  24.2 us (7%)
  matrix products  20.2 us (6%)
    all_gather x1, waiting for transfers between devices, prefix(): everything = jax.tree.map(lambda part: lax.all_gather(part, axis), x)  135 us
    all_gather x1, waiting for transfers between devices, on_device(): value_piece = lax.all_gather(values, 'ctx', axis=0, tiled=True)  41.1 us
    all_gather x1, waiting for transfers between devices, on_device(): key_piece = lax.all_gather(keys, 'ctx', axis=0, tiled=True)  29.8 us
    all_gather x1, blocking collectives, prefix(): everything = jax.tree.map(lambda part: lax.all_gather(part, axis), x)  24.4 us
    select_n x8, other arithmetic, hop(): return jax.tree.map(lambda a, b: jnp.where(reached, a, b), new, before)  16.4 us
    dot_general x4, matrix products, attend_block(): jnp.dot(grad_score, key_cols, preferred_element_type=jnp.float32) * scaling  6.85 us
  transfers between devices with their start and end apart: 3, of which 3 were waited for; matrix products, arithmetic and copies ran while one was open for 9% of the time, Pallas kernels for 0%

commit v1 on v0

--- a/solution.py
+++ b/solution.py
@@ -95,7 +95,12 @@
     row_ids = jnp.arange(block_rows, dtype=jnp.int32)
     empty = jnp.zeros((3, block_rows, kv_width), jnp.bfloat16)
     picked = (empty, empty)
-    key_piece = lax.all_gather(keys, "ctx", axis=0, tiled=True)
+    ring = [keys]
+    for hop_ in range(7):
+        ring.append(lax.ppermute(ring[-1], "ctx", [(dev, (dev + 1) % 8) for dev in range(8)]))
+    key_piece = jnp.roll(
+        jnp.concatenate(ring[::-1], axis=0), (lax.axis_index("ctx") + 1) * ring[0].shape[0], axis=0
+    )
     value_piece = lax.all_gather(values, "ctx", axis=0, tiled=True)
     piece_rows = key_piece.shape[0]
     for slot_number in range(3):

time: 331 us -> 309 us (0.934)
  waiting for transfers between devices: 208 us -> 176 us
  local copies, waits for them, and re-layouts: 25.5 us -> 32.4 us
  blocking collectives: 24.4 us -> 19.5 us
    all_gather x1, waiting for transfers between devices: 41.1 us -> 0.02 us  [on_device(): value_piece = lax.all_gather(values, 'ctx', axis=0, tiled=True)]
    ppermute x0 -> x7, waiting for transfers between devices: none -> 38.6 us  [on_device(): lax.ppermute(ring[-1], 'ctx', [(dev, (dev + 1) % 8) for dev in range(8)])]
    all_gather x1 -> x0, waiting for transfers between devices: 29.8 us -> none  [on_device(): key_piece = lax.all_gather(keys, 'ctx', axis=0, tiled=True)]
    unnamed x57 -> x86, local copies, waits for them, and re-layouts: 1.2 us -> 8.68 us
    all_gather x1, blocking collectives: 24.4 us -> 19.5 us  [prefix(): everything = jax.tree.map(lambda part: lax.all_gather(part, axis), x)]
  transfers between devices with their start and end apart: 3 -> 9, of which waited for: 3 -> 8; matrix products, arithmetic and copies ran while one was open for 9% -> 12% of each run, Pallas kernels for 0% -> 0%
where the time goes in v1:
time: 309 us; the launch traced here: 307 us
  waiting for transfers between devices  176 us (57%)
  local copies, waits for them, and re-layouts  32.4 us (10%)
  other arithmetic  28.7 us (9%)
  between operations  24.3 us (8%)
  matrix products  22.4 us (7%)
  blocking collectives  19.5 us (6%)
  starting transfers between devices  3.25 us (1%)
    all_gather x1, waiting for transfers between devices, prefix(): everything = jax.tree.map(lambda part: lax.all_gather(part, axis), x)  137 us
    ppermute x7, waiting for transfers between devices, on_device(): lax.ppermute(ring[-1], 'ctx', [(dev, (dev + 1) % 8) for dev in range(8)])  38.6 us
    all_gather x1, blocking collectives, prefix(): everything = jax.tree.map(lambda part: lax.all_gather(part, axis), x)  19.5 us
    select_n x8, other arithmetic, hop(): return jax.tree.map(lambda a, b: jnp.where(reached, a, b), new, before)  16.4 us
    unnamed x86, local copies, waits for them, and re-layouts  8.68 us
    dot_general x8, matrix products, dot_rows(): lax.dot_general(left, right, (((1,), (1,)), ((), ())), preferred_element_...  8.21 us
    dot_general x4, matrix products, attend_block(): jnp.dot(grad_score, key_cols, preferred_element_type=jnp.float32) * scaling  6.86 us
  transfers between devices with their start and end apart: 9, of which 8 were waited for; matrix products, arithmetic and copies ran while one was open for 12% of the time, Pallas kernels for 0%

profile of v1, /device:TPU:0, one launch (start us, length us, event | category | flops | bytes accessed | tf_op | source)
XLA Modules:
  0.0 307.2 jit_solution(5131490607370535341)
XLA Ops:
  7.2 3.0 collective-permute-start
  17.3 7.5 %collective-permute-done.1 = bf16[128,512]{1,0:T(8,128)(2,1)S(1)} collective-permute-done((bf16[128,512]{1,0:T(8,128)(2,1)S(1)}, bf16[128,512]{1,0:T(8,128)(2,1)S(1)}, u32[]{:S(2)}, u32[]{:S(2)}) %collective-permute-start.1) | collective-permute-done | bytes 131104 | tf_op jit(solution)/shard_map/ppermute | solution.py:100
  29.3 4.0 %collective-permute-done.2 = bf16[128,512]{1,0:T(8,128)(2,1)S(1)} collective-permute-done((bf16[128,512]{1,0:T(8,128)(2,1)S(1)}, bf16[128,512]{1,0:T(8,128)(2,1)S(1)}, u32[]{:S(2)}, u32[]{:S(2)}) %collective-permute-start.2) | collective-permute-done | bytes 131104 | tf_op jit(solution)/shard_map/ppermute | solution.py:100
  33.4 7.7 %collective-permute-done.3 = bf16[128,512]{1,0:T(8,128)(2,1)S(1)} collective-permute-done((bf16[128,512]{1,0:T(8,128)(2,1)S(1)}, bf16[128,512]{1,0:T(8,128)(2,1)S(1)}, u32[]{:S(2)}, u32[]{:S(2)}) %collective-permute-start.3) | collective-permute-done | bytes 131104 | tf_op jit(solution)/shard_map/ppermute | solution.py:100
  41.9 7.6 %collective-permute-done.4 = bf16[128,512]{1,0:T(8,128)(2,1)} collective-permute-done((bf16[128,512]{1,0:T(8,128)(2,1)S(1)}, bf16[128,512]{1,0:T(8,128)(2,1)}, u32[]{:S(2)}, u32[]{:S(2)}) %collective-permute-start.4) | collective-permute-done | bytes 131104 | tf_op jit(solution)/shard_map/ppermute | solution.py:100
  50.3 1.8 reshape.481
  54.6 3.7 %collective-permute-done.5 = bf16[128,512]{1,0:T(8,128)(2,1)} collective-permute-done((bf16[128,512]{1,0:T(8,128)(2,1)}, bf16[128,512]{1,0:T(8,128)(2,1)}, u32[]{:S(2)}, u32[]{:S(2)}) %collective-permute-start.5) | collective-permute-done | bytes 131104 | tf_op jit(solution)/shard_map/ppermute | solution.py:100
  59.6 6.6 %collective-permute-done.6 = bf16[128,512]{1,0:T(8,128)(2,1)} collective-permute-done((bf16[128,512]{1,0:T(8,128)(2,1)}, bf16[128,512]{1,0:T(8,128)(2,1)}, u32[]{:S(2)}, u32[]{:S(2)}) %collective-permute-start.6) | collective-permute-done | bytes 131104 | tf_op jit(solution)/shard_map/ppermute | solution.py:100
  73.0 3.3 %conditional.3 = (bf16[3,128,512]{2,1,0:T(8,128)(2,1)S(1)}, bf16[3,128,512]{2,1,0:T(8,128)(2,1)S(1)}) conditional(s32[]{:T(128)} %convert_element_type.109, () %tuple.88, (s32[]{:T(128)}, s32[128]{0:T(128)S(1)}, bf16[1024,512]{1,0:T(8,128)(2,1)S(1)}, bf16[1024,512]{1,0:T(8,128)(2,1)}) %tuple.89), branch_computations={%region_1.2_spmd, %region_2.3_spmd} | conditional | flops 133248 | bytes 2104604 | solution.py:125
  73.1 2.2 gather_fusion.1
  78.4 1.7 fusion.48
  94.5 1.6 copy.47
  96.7 1.7 convolution_multiply_fusion.5
  103.2 19.5 %all-gather.1 = f32[8,1,3]{2,1,0:T(1,128)S(1)} all-gather(f32[1,1,3]{2,1,0:T(1,128)S(1)} %fusion.44), channel_id=1, replica_groups=mesh['leaf'=4,'ctx'=8] {'ctx'}, dimensions={0}, use_global_device_ids=true | all-gather | bytes 108 | tf_op jit(solution)/shard_map/all_gather | solution.py:14
  125.3 1.8 reshape.480
  127.1 1.8 reshape.478
  128.8 1.8 reshape.476
  130.6 1.7 fusion.12
  133.2 1.7 fusion.11
  135.7 1.7 fusion.10
  138.2 1.7 fusion.9
  140.8 2.3 pad_maximum_fusion.1
  144.2 137.4 %all-gather.7.cloned.1.call-done = f32[24,2,128,512]{3,2,1,0:T(8,128)} async-done(((f32[3,2,128,512]{3,2,1,0:T(8,128)}), f32[24,2,128,512]{3,2,1,0:T(8,128)}) %all-gather.7.cloned.1.call-update) | async-done | bytes 12582928 | tf_op jit(solution)/shard_map/all_gather | solution.py:14
  281.6 16.8 %while.22 = (s32[]{:T(128)}, f32[3,2,128,512]{3,2,1,0:T(8,128)S(1)}, s32[]{:T(128)}, f32[8,3]{1,0:T(8,128)S(1)}, f32[8,3,2,128,512]{4,3,2,1,0:T(8,128)}, /*index=5*/s32[]{:T(128)}, s32[]{:T(128)}, s32[]{:T(128)}, s32[]{:T(128)}) while((s32[]{:T(128)}, f32[3,2,128,512]{3,2,1,0:T(8,128)S(1)}, s32[]{:T(128)}, ...), condition=%wide.region_20.21_spmd.clone, body=%wide.region_19.20_spmd.clone.sunk | while | flops 1572875 | bytes 4718785 | solution.py:25
  281.6 2.0 fusion.77
  283.7 2.1 fusion.77
  285.8 2.1 fusion.77
  287.9 2.1 fusion.77
  290.0 2.1 fusion.77
  292.1 2.1 fusion.77
  294.2 2.1 fusion.77
  296.3 2.1 fusion.77
  (189 shorter events, 45.6 us)
Async XLA Ops:
  7.2 10.0 %copy-start.34 = (s32[8,4]{0,1:T(4,128)S(1)}, s32[8,4]{0,1:T(4,128)}, u32[]{:S(2)}) copy-start(s32[8,4]{0,1:T(4,128)} %param.30) | copy-start | bytes 388
  7.2 42.4 %copy-start.22 = (bf16[128,4096]{1,0:T(8,128)(2,1)S(1)}, bf16[128,4096]{1,0:T(8,128)(2,1)}, u32[]{:S(2)}) copy-start(bf16[128,4096]{1,0:T(8,128)(2,1)} %param.26) | copy-start | bytes 3145732
  7.2 65.8 %all-gather.5.cloned.1.call-start = ((), (), s32[]{:S(2)}) async-start(), calls=%async_computation | async-start | bytes 1179648 | tf_op jit(solution)/shard_map/all_gather | solution.py:104
  7.2 9.8 %collective-permute-start = (bf16[128,512]{1,0:T(8,128)(2,1)}, bf16[128,512]{1,0:T(8,128)(2,1)S(1)}, u32[]{:S(2)}, u32[]{:S(2)}) collective-permute-start(bf16[128,512]{1,0:T(8,128)(2,1)} %param.27), channel_id=1, source_target_pairs={{0,1},{1,2},{2,3},{3,4},{4,5},{5,6},{6,7},{7,0},{8,9},{9,10},{10,1... | collective-permute-start | bytes 393224 | tf_op jit(solution)/shard_map/ppermute | solution.py:100
  10.3 271.3 %all-gather.7.cloned.1.call-start = ((), (), s32[]{:S(2)}) async-start(), calls=%async_computation.1 | async-start | bytes 14155776 | tf_op jit(solution)/shard_map/all_gather | solution.py:14
  17.0 7.8 %collective-permute-start.1 = (bf16[128,512]{1,0:T(8,128)(2,1)S(1)}, bf16[128,512]{1,0:T(8,128)(2,1)S(1)}, u32[]{:S(2)}, u32[]{:S(2)}) collective-permute-start(bf16[128,512]{1,0:T(8,128)(2,1)S(1)} %collective-permute-done), channel_id=1, source_target_pairs={{0,1},{1,2},{2,3},{3,4},{4,5},{5,6},{6,7},{7,0},{8,9},{9,10},{10,1... | collective-permute-start | bytes 393224 | tf_op jit(solution)/shard_map/ppermute | solution.py:100
  24.8 16.3 %copy-start.28 = (bf16[128,512]{1,0:T(8,128)(2,1)}, bf16[128,512]{1,0:T(8,128)(2,1)S(1)}, u32[]{:S(2)}) copy-start(bf16[128,512]{1,0:T(8,128)(2,1)S(1)} %collective-permute-done.1) | copy-start | bytes 393220
  24.8 8.5 %collective-permute-start.2 = (bf16[128,512]{1,0:T(8,128)(2,1)S(1)}, bf16[128,512]{1,0:T(8,128)(2,1)S(1)}, u32[]{:S(2)}, u32[]{:S(2)}) collective-permute-start(bf16[128,512]{1,0:T(8,128)(2,1)S(1)} %collective-permute-done.1), channel_id=1, source_target_pairs={{0,1},{1,2},{2,3},{3,4},{4,5},{5,6},{6,7},{7,0},{8,9},{9,10},{10,1... | collective-permute-start | bytes 393224 | tf_op jit(solution)/shard_map/ppermute | solution.py:100
  33.3 7.7 %copy-start.30 = (bf16[128,512]{1,0:T(8,128)(2,1)}, bf16[128,512]{1,0:T(8,128)(2,1)S(1)}, u32[]{:S(2)}) copy-start(bf16[128,512]{1,0:T(8,128)(2,1)S(1)} %collective-permute-done.2) | copy-start | bytes 393220
  33.3 7.7 %collective-permute-start.3 = (bf16[128,512]{1,0:T(8,128)(2,1)S(1)}, bf16[128,512]{1,0:T(8,128)(2,1)S(1)}, u32[]{:S(2)}, u32[]{:S(2)}) collective-permute-start(bf16[128,512]{1,0:T(8,128)(2,1)S(1)} %collective-permute-done.2), channel_id=1, source_target_pairs={{0,1},{1,2},{2,3},{3,4},{4,5},{5,6},{6,7},{7,0},{8,9},{9,10},{10,1... | collective-permute-start | bytes 393224 | tf_op jit(solution)/shard_map/ppermute | solution.py:100
  41.1 8.5 %copy-start.32 = (bf16[128,512]{1,0:T(8,128)(2,1)}, bf16[128,512]{1,0:T(8,128)(2,1)S(1)}, u32[]{:S(2)}) copy-start(bf16[128,512]{1,0:T(8,128)(2,1)S(1)} %collective-permute-done.3) | copy-start | bytes 393220
  41.1 8.5 %collective-permute-start.4 = (bf16[128,512]{1,0:T(8,128)(2,1)S(1)}, bf16[128,512]{1,0:T(8,128)(2,1)}, u32[]{:S(2)}, u32[]{:S(2)}) collective-permute-start(bf16[128,512]{1,0:T(8,128)(2,1)S(1)} %collective-permute-done.3), channel_id=1, source_target_pairs={{0,1},{1,2},{2,3},{3,4},{4,5},{5,6},{6,7},{7,0},{8,9},{9,10},{10,1... | collective-permute-start | bytes 393224 | tf_op jit(solution)/shard_map/ppermute | solution.py:100
  49.5 8.8 %collective-permute-start.5 = (bf16[128,512]{1,0:T(8,128)(2,1)}, bf16[128,512]{1,0:T(8,128)(2,1)}, u32[]{:S(2)}, u32[]{:S(2)}) collective-permute-start(bf16[128,512]{1,0:T(8,128)(2,1)} %collective-permute-done.4), channel_id=1, source_target_pairs={{0,1},{1,2},{2,3},{3,4},{4,5},{5,6},{6,7},{7,0},{8,9},{9,10},{10,1... | collective-permute-start | bytes 393224 | tf_op jit(solution)/shard_map/ppermute | solution.py:100
  58.3 8.0 %collective-permute-start.6 = (bf16[128,512]{1,0:T(8,128)(2,1)}, bf16[128,512]{1,0:T(8,128)(2,1)}, u32[]{:S(2)}, u32[]{:S(2)}) collective-permute-start(bf16[128,512]{1,0:T(8,128)(2,1)} %collective-permute-done.5), channel_id=1, source_target_pairs={{0,1},{1,2},{2,3},{3,4},{4,5},{5,6},{6,7},{7,0},{8,9},{9,10},{10,1... | collective-permute-start | bytes 393224 | tf_op jit(solution)/shard_map/ppermute | solution.py:100
  58.4 11.6 %copy-start.31 = (bf16[128,512]{1,0:T(8,128)(2,1)S(1)}, bf16[128,512]{1,0:T(8,128)(2,1)}, u32[]{:S(2)}) copy-start(bf16[128,512]{1,0:T(8,128)(2,1)} %copy-done.30) | copy-start | bytes 393220
  58.4 11.6 %copy-start.29 = (bf16[128,512]{1,0:T(8,128)(2,1)S(1)}, bf16[128,512]{1,0:T(8,128)(2,1)}, u32[]{:S(2)}) copy-start(bf16[128,512]{1,0:T(8,128)(2,1)} %copy-done.28) | copy-start | bytes 393220
  58.4 11.6 %copy-start.21 = (bf16[128,512]{1,0:T(8,128)(2,1)S(1)}, bf16[128,512]{1,0:T(8,128)(2,1)}, u32[]{:S(2)}) copy-start(bf16[128,512]{1,0:T(8,128)(2,1)} %param.27) | copy-start | bytes 393220
  58.7 28.5 %copy-start.6 = (bf16[1024,128]{1,0:T(8,128)(2,1)}, bf16[1024,128]{1,0:T(8,128)(2,1)S(1)}, u32[]{:S(2)}) copy-start(bf16[1024,128]{1,0:T(8,128)(2,1)S(1)} %reshape.487) | copy-start | bytes 786436
  58.7 14.1 %copy-start.33 = (bf16[128,512]{1,0:T(8,128)(2,1)S(1)}, bf16[128,512]{1,0:T(8,128)(2,1)}, u32[]{:S(2)}) copy-start(bf16[128,512]{1,0:T(8,128)(2,1)} %copy-done.32) | copy-start | bytes 393220
  78.4 5.5 %copy-start.7 = (bf16[512,512]{1,0:T(8,128)(2,1)}, bf16[512,512]{1,0:T(8,128)(2,1)S(1)}, u32[]{:S(2)}) copy-start(bf16[512,512]{1,0:T(8,128)(2,1)S(1)} %constant_dynamic-update-slice_fusion.16) | copy-start | bytes 1572868
  81.1 4.9 %copy-start.10 = (bf16[1024,128]{1,0:T(8,128)(2,1)}, bf16[1024,128]{1,0:T(8,128)(2,1)S(1)}, u32[]{:S(2)}) copy-start(bf16[1024,128]{1,0:T(8,128)(2,1)S(1)} %convolution_convert_fusion) | copy-start | bytes 786436
  82.5 4.7 %copy-start.12 = (bf16[1024,128]{1,0:T(8,128)(2,1)}, bf16[1024,128]{1,0:T(8,128)(2,1)S(1)}, u32[]{:S(2)}) copy-start(bf16[1024,128]{1,0:T(8,128)(2,1)S(1)} %convolution_convert_fusion.1) | copy-start | bytes 786436
  84.0 5.4 %copy-start.13 = (bf16[1024,128]{1,0:T(8,128)(2,1)}, bf16[1024,128]{1,0:T(8,128)(2,1)S(1)}, u32[]{:S(2)}) copy-start(bf16[1024,128]{1,0:T(8,128)(2,1)S(1)} %convolution_convert_fusion.2) | copy-start | bytes 786436
  85.4 6.3 %copy-start.14 = (bf16[1024,128]{1,0:T(8,128)(2,1)}, bf16[1024,128]{1,0:T(8,128)(2,1)S(1)}, u32[]{:S(2)}) copy-start(bf16[1024,128]{1,0:T(8,128)(2,1)S(1)} %convolution_convert_fusion.3) | copy-start | bytes 786436
  86.7 9.4 %copy-start.1 = (bf16[1024,512]{0,1:T(8,128)(2,1)}, bf16[1024,512]{0,1:T(8,128)(2,1)S(1)}, u32[]{:S(2)}) copy-start(bf16[1024,512]{0,1:T(8,128)(2,1)S(1)} %multiply_convert_fusion) | copy-start | bytes 3145732
  88.9 7.7 %copy-start.2 = (bf16[1024,512]{0,1:T(8,128)(2,1)}, bf16[1024,512]{0,1:T(8,128)(2,1)S(1)}, u32[]{:S(2)}) copy-start(bf16[1024,512]{0,1:T(8,128)(2,1)S(1)} %multiply_convert_fusion.1) | copy-start | bytes 3145732
  96.1 2.7 copy-start.4
  96.1 2.7 copy-start.20
  99.8 24.7 %copy-start.11 = (bf16[1024,128]{1,0:T(8,128)(2,1)S(1)}, bf16[1024,128]{1,0:T(8,128)(2,1)}, u32[]{:S(2)}) copy-start(bf16[1024,128]{1,0:T(8,128)(2,1)} %copy-done.10) | copy-start | bytes 786436
  101.1 29.5 %copy-start.8 = (bf16[512,512]{1,0:T(8,128)(2,1)S(1)}, bf16[512,512]{1,0:T(8,128)(2,1)}, u32[]{:S(2)}) copy-start(bf16[512,512]{1,0:T(8,128)(2,1)} %copy-done.7) | copy-start | bytes 1572868
  140.0 3.1 %copy-start.23 = (bf16[128,1024]{1,0:T(8,128)(2,1)S(1)}, bf16[128,1024]{1,0:T(8,128)(2,1)}, u32[]{:S(2)}) copy-start(bf16[128,1024]{1,0:T(8,128)(2,1)} %reshape.490) | copy-start | bytes 786436
  140.0 3.1 %copy-start.24 = (bf16[128,1024]{1,0:T(8,128)(2,1)S(1)}, bf16[128,1024]{1,0:T(8,128)(2,1)}, u32[]{:S(2)}) copy-start(bf16[128,1024]{1,0:T(8,128)(2,1)} %reshape.488) | copy-start | bytes 786436
  (12 other events, 20.6 us)
Sparse Core Ops, SparseCore 0:
  10.4 44.7 all-gather.4
  101.2 180.3 all-gather.6
